TPU v7x, 32 devices: a whole 2x2x4 slice. The times are simulated.
32 devices in a mesh: row: 2 (over x), col: 16 (over z, y, core).
Axes of the slice: x: 2, y: 2, z: 4, core: 2. Of those that a mesh axis runs over, the one named last changes fastest.
Arguments:
- panel: bfloat16 [49152, 1024], P('col', 'row'), may hold values from -0.1875 to 0.1875
- rhs: float32 [1024, 49152], P('row', 'col'), may hold values from -6 to 6
- diag_inverse: bfloat16 [2, 512, 512], replicated, may hold values from -1 to 2, as said below
Outputs:
- solved: bfloat16 [1024, 1024], P(None, 'row')
- updated: float32 [1024, 49152], P('row', 'col')
Inputs may be any that keep to these rules, and one draw needn't show every extreme that they name: `diag_inverse`: each block is lower triangular; its diagonal entries are 0.5 or more.
All inputs are finite; a program needn't handle non-finite values.
Results may differ from a plain program's by a relative error of at most 0.0065.
Values may be sent and summed in bfloat16 or wider, within the bound.
A program may use at most 128 MiB of HBM per device.

v0:
```python
import jax
import jax.numpy as jnp
from jax import lax
from jax.sharding import PartitionSpec as P


def spread(value, axis, root):
    mine = lax.axis_index(axis) == root
    return lax.psum(jnp.where(mine, value, jnp.zeros_like(value)), axis)


def spread_block(values, owner):
    return spread(values, "col", owner)


def shards(panel, rhs, diag_inverse):
    block_size = diag_inverse.shape[1]
    step_count = diag_inverse.shape[0]
    slice_count = rhs.shape[0]
    rhs_count = slice_count * lax.axis_size("row")
    row_index = lax.axis_index("row")
    col_index = lax.axis_index("col")
    dropped = (col_index < step_count) & (row_index >= col_index)
    top_block = jnp.where(dropped, jnp.zeros_like(panel[:block_size]), panel[:block_size])
    masked = jnp.concatenate([top_block, panel[block_size:]], axis=0)
    contract = (((1,), (1,)), ((), ()))
    own_solved = jnp.zeros((rhs_count, block_size), jnp.bfloat16)
    for current in range(step_count):
        inverse = diag_inverse[current].astype(jnp.float32)
        partial_value = lax.cond(
            col_index == current,
            lambda: lax.dot_general(
                own_solved, masked[:block_size], contract, preferred_element_type=jnp.float32
            ),
            lambda: jnp.zeros((rhs_count, block_size), jnp.float32),
        )
        shares = lax.psum_scatter(partial_value, "row", scatter_dimension=0, tiled=True)
        residual = rhs[:, :block_size] - shares
        solution = jnp.dot(residual, inverse.T, precision=lax.Precision.HIGHEST).astype(
            jnp.bfloat16
        )
        share_arrived = spread_block(solution, current)
        arrived = lax.all_gather(share_arrived, "row", axis=0, tiled=True)
        own_solved = jnp.where(row_index == current, arrived, own_solved)
    reduced = lax.psum_scatter(
        lax.dot_general(own_solved, masked, contract, preferred_element_type=jnp.float32).astype(
            jnp.bfloat16
        ),
        "row",
        scatter_dimension=0,
        tiled=True,
    ).astype(jnp.float32)
    updated = rhs - reduced
    return (own_solved, updated)


def solution(mesh):
    placed = (P("col", "row"), P("row", "col"), P())
    return jax.shard_map(
        shards,
        mesh=mesh,
        in_specs=placed,
        out_specs=(P(None, "row"), P("row", "col")),
        check_vma=False,
    )
```

profile of v0, /device:TPU:12, one launch (start us, length us, event | category | flops | bytes accessed | tf_op | source)
XLA Modules:
  0.0 414.7 jit_solution(9032343016565336060)
XLA Ops:
  7.2 1.1 slice_select_fusion
  8.3 0.3 conditional.2
  8.3 0.2 broadcast.6
  8.6 1.3 copy-done
  9.9 0.0 all-reduce.3.cloned.1.call-start
  10.0 33.9 %reduce-scatter.4.cloned.1.call-done = f32[512,512]{1,0:T(8,128)} async-done(((f32[1024,512]{1,0:T(8,128)}), f32[512,512]{1,0:T(8,128)}) %reduce-scatter.4.cloned.1.call-update) | async-done | bytes 1048592 | tf_op jit(solution)/shard_map/reduce_scatter | solution.py:37
  43.8 3.5 fusion.6
  47.4 0.0 all-gather.3.cloned.1.call-start
  47.4 91.6 %all-reduce.3.cloned.1.call-done = bf16[512,512]{1,0:T(8,128)(2,1)} async-done(((bf16[512,512]{1,0:T(8,128)(2,1)}), bf16[512,512]{1,0:T(8,128)(2,1)}) %all-reduce.3.cloned.1.call-update) | async-done | bytes 524304 | tf_op jit(solution)/shard_map/psum | solution.py:9
  139.1 22.8 %all-gather.3.cloned.1.call-done = bf16[1024,512]{1,0:T(8,128)(2,1)} async-done(((bf16[512,512]{1,0:T(8,128)(2,1)}), bf16[1024,512]{1,0:T(8,128)(2,1)}) %all-gather.3.cloned.1.call-update) | async-done | bytes 1048592 | tf_op jit(solution)/shard_map/all_gather | solution.py:43
  161.9 1.3 broadcast_select_fusion
  163.2 0.3 conditional.3
  163.2 0.2 broadcast.7
  163.5 1.3 copy-done.1
  164.8 0.0 all-reduce.5.cloned.1.call-start
  164.8 32.0 %reduce-scatter.6.cloned.1.call-done = f32[512,512]{1,0:T(8,128)} async-done(((f32[1024,512]{1,0:T(8,128)}), f32[512,512]{1,0:T(8,128)}) %reduce-scatter.6.cloned.1.call-update) | async-done | bytes 1048592 | tf_op jit(solution)/shard_map/reduce_scatter | solution.py:37
  196.9 3.5 fusion.7
  200.4 91.5 %all-reduce.5.cloned.1.call-done = bf16[512,512]{1,0:T(8,128)(2,1)} async-done(((bf16[512,512]{1,0:T(8,128)(2,1)}), bf16[512,512]{1,0:T(8,128)(2,1)}) %all-reduce.5.cloned.1.call-update) | async-done | bytes 524304 | tf_op jit(solution)/shard_map/psum | solution.py:9
  292.0 22.6 %all-gather.5.cloned.1.call-done = bf16[1024,512]{1,0:T(8,128)(2,1)} async-done(((bf16[512,512]{1,0:T(8,128)(2,1)}), bf16[1024,512]{1,0:T(8,128)(2,1)}) %all-gather.5.cloned.1.call-update) | async-done | bytes 1048592 | tf_op jit(solution)/shard_map/all_gather | solution.py:43
  314.6 0.1 broadcast_select_fusion.1
  314.7 1.6 slice-done
  316.3 6.2 %convolution_convert_fusion = bf16[1024,3072]{1,0:T(8,128)(2,1)} fusion(bf16[1024,512]{1,0:T(8,128)(2,1)S(1)} %broadcast_select_fusion.1, bf16[2560,512]{1,0:T(8,128)(2,1)S(1)} %slice-done, bf16[512,512]{1,0:T(8,128)(2,1)S(1)} %slice_select_fusion), kind=kOutput, calls=%fused_computation.4 | convolution fusion | flops 3230662656 | bytes 10485760 | tf_op jit(solution)/shard_map/dot_general | solution.py:46
  322.6 77.6 %reduce-scatter.8.cloned.1.call-done = bf16[512,3072]{1,0:T(8,128)(2,1)} async-done(((bf16[1024,3072]{1,0:T(8,128)(2,1)}), bf16[512,3072]{1,0:T(8,128)(2,1)}) %reduce-scatter.8.cloned.1.call-update) | async-done | bytes 3145744 | tf_op jit(solution)/shard_map/reduce_scatter | solution.py:45
  400.2 7.7 %convert_subtract_fusion = f32[512,3072]{1,0:T(8,128)} fusion(f32[512,3072]{1,0:T(8,128)} %param.8, bf16[512,3072]{1,0:T(8,128)(2,1)} %reduce-scatter.8.cloned.1.call-done), kind=kLoop, calls=%fused_computation.3 | loop fusion | flops 3145728 | bytes 15728640 | tf_op jit(solution)/shard_map/sub | solution.py:53
  (18 shorter events, 0.3 us)
Async XLA Ops:
  7.2 36.7 %reduce-scatter.4.cloned.1.call-start = ((), (), s32[]{:S(2)}) async-start(), calls=%async_computation.3 | async-start | bytes 3145728 | tf_op jit(solution)/shard_map/reduce_scatter | solution.py:37
  8.6 1.3 copy-start
  9.9 129.1 %all-reduce.3.cloned.1.call-start = ((), (), s32[]{:S(2)}) async-start(), calls=%async_computation.4 | async-start | bytes 1048576 | tf_op jit(solution)/shard_map/psum | solution.py:9
  47.4 114.5 %all-gather.3.cloned.1.call-start = ((), (), s32[]{:S(2)}) async-start(), calls=%async_computation.5 | async-start | bytes 1572864 | tf_op jit(solution)/shard_map/all_gather | solution.py:43
  139.0 57.8 %reduce-scatter.6.cloned.1.call-start = ((), (), s32[]{:S(2)}) async-start(), calls=%async_computation.6 | async-start | bytes 3145728 | tf_op jit(solution)/shard_map/reduce_scatter | solution.py:37
  163.5 1.3 copy-start.1
  164.8 127.1 %all-reduce.5.cloned.1.call-start = ((), (), s32[]{:S(2)}) async-start(), calls=%async_computation.7 | async-start | bytes 1048576 | tf_op jit(solution)/shard_map/psum | solution.py:9
  200.4 114.2 %copy-start.2 = (bf16[1024,512]{1,0:T(8,128)(2,1)S(1)}, bf16[1024,512]{1,0:T(8,128)(2,1)}, u32[]{:S(2)}) copy-start(bf16[1024,512]{1,0:T(8,128)(2,1)} %all-gather.3.cloned.1.call-done) | copy-start | bytes 3145732
  200.4 114.2 %all-gather.5.cloned.1.call-start = ((), (), s32[]{:S(2)}) async-start(), calls=%async_computation.8 | async-start | bytes 1572864 | tf_op jit(solution)/shard_map/all_gather | solution.py:43
  291.9 108.2 %reduce-scatter.8.cloned.1.call-start = ((), (), s32[]{:S(2)}) async-start(), calls=%async_computation.9 | async-start | bytes 9437184 | tf_op jit(solution)/shard_map/reduce_scatter | solution.py:45
  314.6 1.7 slice-start
  316.3 6.2 %copy-start.3 = (bf16[1024,512]{1,0:T(8,128)(2,1)}, bf16[1024,512]{1,0:T(8,128)(2,1)S(1)}, u32[]{:S(2)}) copy-start(bf16[1024,512]{1,0:T(8,128)(2,1)S(1)} %broadcast_select_fusion.1) | copy-start | bytes 3145732
Sparse Core Ops, SparseCore 0:
  10.8 33.0 reduce-scatter.3
  47.8 91.1 all-reduce.2
  140.6 21.2 all-gather.2
  164.9 31.8 reduce-scatter.5
  200.7 91.1 all-reduce.4
  293.3 21.2 all-gather.4
  322.7 77.4 reduce-scatter.7
where the time goes:
time: 417 us; the launch traced here: 415 us
  waiting for transfers between devices  372 us (89%)
  between operations  14.2 us (3%)
  matrix products  13.2 us (3%)
  other arithmetic  10.2 us (2%)
  local copies, waits for them, and re-layouts  4.76 us (1%)
    psum x2, waiting for transfers between devices, spread(): return lax.psum(jnp.where(mine, value, jnp.zeros_like(value)), axis)  183 us
    reduce_scatter x1, waiting for transfers between devices, shards(): lax.psum_scatter(lax.dot_general(own_solved, masked, contract, preferred_...  77.6 us
    reduce_scatter x2, waiting for transfers between devices, shards(): lax.psum_scatter(partial_value, 'row', scatter_dimension=0, tiled=True)  65.9 us
    all_gather x2, waiting for transfers between devices, shards(): arrived = lax.all_gather(share_arrived, 'row', axis=0, tiled=True)  45.4 us
  transfers between devices with their start and end apart: 7, of which 7 were waited for; matrix products, arithmetic and copies ran while one was open for 0% of the time, Pallas kernels for 0%

commit v1 on v0

v1 whole, which is shorter than its diff:
```python
import functools

import jax
import jax.numpy as jnp
from jax import lax
from jax.experimental import pallas as pl
from jax.experimental.pallas import tpu as pltpu
from jax.sharding import PartitionSpec as P

PIECES = 4
MESH = pl.DeviceIdType.MESH
CONTRACT = (((1,), (1,)), ((), ()))


def times_transposed(left, right):
    return lax.dot_general(left, right, CONTRACT, preferred_element_type=jnp.float32)


def solve(residual, inverse):
    high = residual.astype(jnp.bfloat16)
    rest = residual - high.astype(jnp.float32)
    middle = rest.astype(jnp.bfloat16)
    low = (rest - middle.astype(jnp.float32)).astype(jnp.bfloat16)
    total = times_transposed(low, inverse) + times_transposed(middle, inverse)
    return (total + times_transposed(high, inverse)).astype(jnp.bfloat16)


def kernel(
    cols,
    panel_hbm,
    rhs_hbm,
    inverse_hbm,
    solved_ref,
    updated_ref,
    pan,
    quarter,
    inverse_ref,
    load_panel,
    load_rhs,
    load_inverse,
    panel_send,
    panel_recv,
    piece_send,
    piece_recv,
):
    steps, block = inverse_hbm.shape[0], inverse_hbm.shape[1]
    blocks = panel_hbm.shape[0] // block
    rows = block // PIECES
    chips = cols // 2
    i = lax.axis_index("row")
    c = lax.axis_index("col")
    other = 1 - i
    core = lax.rem(c, 2)
    chip = lax.div(c, 2)
    mate = c + 1 - 2 * core
    root = chip == 0
    is_first = core == 0
    has_child = chip + 2 < chips
    has_second = root & (chips > 1)

    def dropped(k):
        return (c < steps) & (k >= c)

    def rhs_load(j):
        at = pl.ds(pl.multiple_of(j * block, block), block)
        return pltpu.make_async_copy(rhs_hbm.at[:, at], updated_ref.at[:, at], load_rhs.at[j])

    def panel_load(j):
        at = pl.ds(pl.multiple_of(j * block, block), block)
        return pltpu.make_async_copy(panel_hbm.at[at, :], pan.at[i, at, :], load_panel.at[j])

    def panel_copy(j, which):
        at = pl.ds(pl.multiple_of(j * block, block), block)
        return pltpu.make_async_remote_copy(
            src_ref=pan.at[which, at, :],
            dst_ref=pan.at[which, at, :],
            send_sem=panel_send.at[j],
            recv_sem=panel_recv.at[j],
            device_id=(other, c),
            device_id_type=MESH,
        )

    def piece_copy(source, target, p, way, device):
        at = pl.ds(p * rows, rows)
        return pltpu.make_async_remote_copy(
            src_ref=quarter.at[source, at, :],
            dst_ref=quarter.at[target, at, :],
            send_sem=piece_send.at[way, source, p],
            recv_sem=piece_recv.at[target, p],
            device_id=device,
            device_id_type=MESH,
        )

    inverse_load = pltpu.make_async_copy(
        inverse_hbm.at[core], inverse_ref, load_inverse
    )
    rhs_load(0).start()
    inverse_load.start()

    @pl.when(jnp.logical_not(dropped(i)))
    def _():
        panel_load(0).start()

    for j in range(1, blocks):
        panel_load(j).start()
    for j in range(1, blocks):
        rhs_load(j).start()

    barrier = pltpu.get_barrier_semaphore()

    def greet(device):
        pl.semaphore_signal(barrier, inc=1, device_id=device, device_id_type=MESH)

    cross_pair = ((i == 0) & (c == 1)) | ((i == 1) & (c == 0))
    greet((other, c))
    greet((i, mate))

    @pl.when(has_child)
    def _():
        greet((i, c + 4))

    @pl.when(has_second)
    def _():
        greet((i, c + 2))

    @pl.when(chip == 1)
    def _():
        greet((i, c - 2))

    @pl.when(chip >= 2)
    def _():
        greet((i, c - 4))

    @pl.when(cross_pair)
    def _():
        greet((other, 1 - c))

    count = (
        2
        + has_child.astype(jnp.int32)
        + has_second.astype(jnp.int32)
        + (chip >= 1).astype(jnp.int32)
        + cross_pair.astype(jnp.int32)
    )
    pl.semaphore_wait(barrier, count)

    @pl.when(jnp.logical_not(dropped(i)))
    def _():
        panel_load(0).wait()
        panel_copy(0, i).start()

    for k in range(steps):

        @pl.when(dropped(k))
        def _(k=k):
            pan[k, pl.ds(0, block), :] = jnp.zeros((block, block), jnp.bfloat16)

    def send_rest():
        for j in range(1, blocks):
            panel_load(j).wait()
            panel_copy(j, i).start()

    pl.when(jnp.logical_not(root))(send_rest)
    inverse_load.wait()
    rhs_load(0).wait()

    def forward(slot, p):
        piece_copy(slot, slot, p, 0, (i, mate)).start()

        @pl.when(has_child)
        def _():
            piece_copy(slot, slot, p, 1, (i, c + 4)).start()

        @pl.when(has_second)
        def _():
            piece_copy(slot, slot, p, 2, (i, c + 2)).start()

    def forward_sent(slot, p):
        piece_copy(slot, slot, p, 0, (i, mate)).wait_send()

        @pl.when(has_child)
        def _():
            piece_copy(slot, slot, p, 1, (i, c + 4)).wait_send()

        @pl.when(has_second)
        def _():
            piece_copy(slot, slot, p, 2, (i, c + 2)).wait_send()

    def arrived(slot, p):
        piece_copy(slot, slot, p, 0, (i, mate)).wait_recv()

    @pl.when(is_first)
    def _():
        @pl.when(root)
        def _():
            quarter[0] = solve(updated_ref[:, pl.ds(0, block)], inverse_ref[...])
            for p in range(PIECES):

                @pl.when(i == 1)
                def _(p=p):
                    piece_copy(0, 2, p, 3, (other, c)).start()

                forward(0, p)
            send_rest()

        @pl.when(jnp.logical_not(root))
        def _():
            for p in range(PIECES):
                arrived(0, p)
                forward(0, p)

        for p in range(PIECES):
            arrived(2, p)
            forward(2, p)
        for p in range(PIECES):
            arrived(1, p)

    @pl.when(jnp.logical_not(is_first))
    def _():
        @pl.when(root)
        def _():
            for p in range(PIECES):
                arrived(0, p)

            @pl.when(i == 1)
            def _():
                panel_copy(0, other).wait_recv()

            residual = updated_ref[:, pl.ds(0, block)] - times_transposed(
                quarter[0], pan[0, pl.ds(0, block), :]
            )
            quarter[1] = solve(residual, inverse_ref[...])
            for p in range(PIECES):

                @pl.when(i == 0)
                def _(p=p):
                    piece_copy(1, 2, p, 3, (other, 1 - c)).start()

                forward(1, p)
            send_rest()

        @pl.when(jnp.logical_not(root))
        def _():
            for p in range(PIECES):
                arrived(1, p)
                forward(1, p)
            for p in range(PIECES):
                arrived(0, p)

        for p in range(PIECES):
            arrived(2, p)

    solved_ref[pl.ds(pl.multiple_of(i * block, block), block), :] = quarter[i]
    solved_ref[pl.ds(pl.multiple_of(other * block, block), block), :] = quarter[2]

    early = (c == 1) & (i == 1)

    @pl.when(jnp.logical_not(dropped(other)) & jnp.logical_not(early))
    def _():
        panel_copy(0, other).wait_recv()

    def update(j):
        at = pl.ds(pl.multiple_of(j * block, block), block)
        total = times_transposed(quarter[0], pan[0, at, :])
        total = total + times_transposed(quarter[1], pan[1, at, :])
        updated_ref[:, at] = updated_ref[:, at] - total

    update(0)

    def chunk(j, carry):
        rhs_load(j).wait()
        panel_copy(j, other).wait_recv()
        update(j)
        return carry

    lax.fori_loop(1, blocks, chunk, 0)

    @pl.when(jnp.logical_not(dropped(i)))
    def _():
        panel_copy(0, i).wait_send()

    for j in range(1, blocks):
        panel_copy(j, i).wait_send()
    for p in range(PIECES):

        @pl.when(is_first)
        def _(p=p):
            forward_sent(0, p)
            forward_sent(2, p)

            @pl.when(root & (i == 1))
            def _():
                piece_copy(0, 2, p, 3, (other, c)).wait_send()

        @pl.when(jnp.logical_not(is_first))
        def _(p=p):
            forward_sent(1, p)

            @pl.when(root & (i == 0))
            def _():
                piece_copy(1, 2, p, 3, (other, 1 - c)).wait_send()


def shards(panel, rhs, diag_inverse):
    steps, block = diag_inverse.shape[:2]
    blocks = panel.shape[0] // block
    return pl.pallas_call(
        functools.partial(kernel, lax.axis_size("col")),
        out_shape=(
            pltpu.VMEM((steps * block, block), jnp.bfloat16),
            pltpu.VMEM(rhs.shape, jnp.float32),
        ),
        in_specs=[pl.BlockSpec(memory_space=pltpu.HBM)] * 3,
        out_specs=(pl.BlockSpec(memory_space=pltpu.VMEM),) * 2,
        scratch_shapes=[
            pltpu.VMEM((steps,) + panel.shape, jnp.bfloat16),
            pltpu.VMEM((3, block, block), jnp.bfloat16),
            pltpu.VMEM((block, block), jnp.bfloat16),
            pltpu.SemaphoreType.DMA((blocks,)),
            pltpu.SemaphoreType.DMA((blocks,)),
            pltpu.SemaphoreType.DMA,
            pltpu.SemaphoreType.DMA((blocks,)),
            pltpu.SemaphoreType.DMA((blocks,)),
            pltpu.SemaphoreType.DMA((4, 3, PIECES)),
            pltpu.SemaphoreType.DMA((3, PIECES)),
        ],
        compiler_params=pltpu.CompilerParams(
            collective_id=0, has_side_effects=True, vmem_limit_bytes=56 * 1024 * 1024
        ),
    )(panel, rhs, diag_inverse)


def solution(mesh):
    placed = (P("col", "row"), P("row", "col"), P())
    return jax.shard_map(
        shards,
        mesh=mesh,
        in_specs=placed,
        out_specs=(P(None, "row"), P("row", "col")),
        check_vma=False,
    )
```

time: 417 us -> 77.6 us (0.19)
  waiting for transfers between devices: 372 us -> 0 us
  Pallas kernels: 0 us -> 73.1 us
  between operations: 14.2 us -> 0.64 us
  matrix products: 13.2 us -> 0 us
  other arithmetic: 10.2 us -> 0 us
    psum x2 -> x0, waiting for transfers between devices: 183 us -> none  [spread(): return lax.psum(jnp.where(mine, value, jnp.zeros_like(value)), axis)]
    reduce_scatter x3 -> x0, waiting for transfers between devices: 143 us -> none  [the longest x1 77.6 us: shards(): lax.psum_scatter(lax.dot_general(own_solved, masked, contract, preferred_...]
    pallas_call x0 -> x1, Pallas kernels: none -> 73.1 us  [shards(): pl.pallas_call(functools.partial(kernel, lax.axis_size('col')), out_shape...]
    all_gather x2 -> x0, waiting for transfers between devices: 45.4 us -> none  [shards(): arrived = lax.all_gather(share_arrived, 'row', axis=0, tiled=True)]
    dot_general x3 -> x0, matrix products: 13.2 us -> none  [the longest x2 6.99 us: shards(): jnp.dot(residual, inverse.T, precision=lax.Precision.HIGHEST)]
    sub x1 -> x0, other arithmetic: 7.7 us -> none  [shards(): updated = rhs - reduced]
  transfers between devices with their start and end apart: 7 -> 0, of which waited for: 7 -> 0; matrix products, arithmetic and copies ran while one was open for 0% -> 0% of each run, Pallas kernels for 0% -> 0%
where the time goes in v1:
time: 77.6 us; the launch traced here: 77.5 us
  Pallas kernels  73.1 us (94%)
  local copies, waits for them, and re-layouts  3.68 us (5%)
    pallas_call x1, Pallas kernels, shards(): pl.pallas_call(functools.partial(kernel, lax.axis_size('col')), out_shape...  73.1 us
    unnamed x2, local copies, waits for them, and re-layouts  3.68 us

profile of v1, /device:TPU:12, one launch (start us, length us, event | category | flops | bytes accessed | tf_op | source)
XLA Modules:
  0.0 77.5 jit_solution(1021214785879107884)
XLA Ops:
  0.6 73.1 %shard_map.50 = (bf16[1024,512]{1,0:T(8,128)(2,1)S(1)}, f32[512,3072]{1,0:T(8,128)S(1)}) custom-call(bf16[3072,512]{1,0:T(8,128)(2,1)} %panel_hbm.1, f32[512,3072]{1,0:T(8,128)} %rhs_hbm.1, bf16[2,512,512]{2,1,0:T(8,128)(2,1)} %inverse_hbm.1), custom_call_target="tpu_custom_call" | custom-call | tf_op jit(solution)/shard_map/pallas_call | solution.py:307
  73.8 1.0 %copy.7 = bf16[1024,512]{1,0:T(8,128)(2,1)} copy(bf16[1024,512]{1,0:T(8,128)(2,1)S(1)} %get-tuple-element.2) | data formatting | bytes 2097152
  74.8 2.7 %copy.8 = f32[512,3072]{1,0:T(8,128)} copy(f32[512,3072]{1,0:T(8,128)S(1)} %get-tuple-element.3) | data formatting | bytes 12582912

commit v2 on v1

--- a/solution.py
+++ b/solution.py
@@ -30,7 +30,6 @@
     panel_hbm,
     rhs_hbm,
     inverse_hbm,
-    solved_ref,
     updated_ref,
     pan,
     quarter,
@@ -91,6 +90,35 @@
             device_id_type=MESH,
         )
 
+    barrier = pltpu.get_barrier_semaphore()
+
+    def greet(device):
+        pl.semaphore_signal(barrier, inc=1, device_id=device, device_id_type=MESH)
+
+    cross_pair = ((i == 0) & (c == 1)) | ((i == 1) & (c == 0))
+    greet((other, c))
+    greet((i, mate))
+
+    @pl.when(has_child)
+    def _():
+        greet((i, c + 4))
+
+    @pl.when(has_second)
+    def _():
+        greet((i, c + 2))
+
+    @pl.when(chip == 1)
+    def _():
+        greet((i, c - 2))
+
+    @pl.when(chip >= 2)
+    def _():
+        greet((i, c - 4))
+
+    @pl.when(cross_pair)
+    def _():
+        greet((other, 1 - c))
+
     inverse_load = pltpu.make_async_copy(
         inverse_hbm.at[core], inverse_ref, load_inverse
     )
@@ -105,35 +133,6 @@
         panel_load(j).start()
     for j in range(1, blocks):
         rhs_load(j).start()
-
-    barrier = pltpu.get_barrier_semaphore()
-
-    def greet(device):
-        pl.semaphore_signal(barrier, inc=1, device_id=device, device_id_type=MESH)
-
-    cross_pair = ((i == 0) & (c == 1)) | ((i == 1) & (c == 0))
-    greet((other, c))
-    greet((i, mate))
-
-    @pl.when(has_child)
-    def _():
-        greet((i, c + 4))
-
-    @pl.when(has_second)
-    def _():
-        greet((i, c + 2))
-
-    @pl.when(chip == 1)
-    def _():
-        greet((i, c - 2))
-
-    @pl.when(chip >= 2)
-    def _():
-        greet((i, c - 4))
-
-    @pl.when(cross_pair)
-    def _():
-        greet((other, 1 - c))
 
     count = (
         2
@@ -250,9 +249,6 @@
         for p in range(PIECES):
             arrived(2, p)
 
-    solved_ref[pl.ds(pl.multiple_of(i * block, block), block), :] = quarter[i]
-    solved_ref[pl.ds(pl.multiple_of(other * block, block), block), :] = quarter[2]
-
     early = (c == 1) & (i == 1)
 
     @pl.when(jnp.logical_not(dropped(other)) & jnp.logical_not(early))
@@ -273,7 +269,9 @@
         update(j)
         return carry
 
-    lax.fori_loop(1, blocks, chunk, 0)
+    lax.fori_loop(1, blocks - 1, chunk, 0)
+    rhs_load(blocks - 1).wait()
+    panel_copy(blocks - 1, other).wait_recv()
 
     @pl.when(jnp.logical_not(dropped(i)))
     def _():
@@ -301,20 +299,56 @@
                 piece_copy(1, 2, p, 3, (other, 1 - c)).wait_send()
 
 
+def writer(updated_ref, pan, quarter, solved_hbm, updated_hbm, last, done_sem, last_sem, solved_sem):
+    block = quarter.shape[1]
+    blocks = updated_ref.shape[1] // block
+    i = lax.axis_index("row")
+    copies = []
+
+    def put(j):
+        at = pl.ds(j * block, block)
+        copies.append(
+            pltpu.make_async_copy(updated_ref.at[:, at], updated_hbm.at[:, at], done_sem.at[j])
+        )
+        copies[-1].start()
+
+    for j in range(blocks - 1):
+        put(j)
+    for part, slot in enumerate((i, 2)):
+        half = i if part == 0 else 1 - i
+        at = pl.ds(pl.multiple_of(half * block, block), block)
+        copies.append(
+            pltpu.make_async_copy(quarter.at[slot], solved_hbm.at[at, :], solved_sem.at[part])
+        )
+        copies[-1].start()
+    width = block // 2
+    for part in range(2):
+        start = (blocks - 1) * block + part * width
+        at = pl.ds(start, width)
+        total = times_transposed(quarter[0], pan[0, at, :])
+        total = total + times_transposed(quarter[1], pan[1, at, :])
+        last[part] = updated_ref[:, at] - total
+        copies.append(
+            pltpu.make_async_copy(last.at[part], updated_hbm.at[:, at], last_sem.at[part])
+        )
+        copies[-1].start()
+    for copy in copies:
+        copy.wait()
+
+
 def shards(panel, rhs, diag_inverse):
     steps, block = diag_inverse.shape[:2]
     blocks = panel.shape[0] // block
-    return pl.pallas_call(
+    parts = pl.pallas_call(
         functools.partial(kernel, lax.axis_size("col")),
         out_shape=(
-            pltpu.VMEM((steps * block, block), jnp.bfloat16),
             pltpu.VMEM(rhs.shape, jnp.float32),
+            pltpu.VMEM((steps,) + panel.shape, jnp.bfloat16),
+            pltpu.VMEM((3, block, block), jnp.bfloat16),
         ),
         in_specs=[pl.BlockSpec(memory_space=pltpu.HBM)] * 3,
-        out_specs=(pl.BlockSpec(memory_space=pltpu.VMEM),) * 2,
+        out_specs=(pl.BlockSpec(memory_space=pltpu.VMEM),) * 3,
         scratch_shapes=[
-            pltpu.VMEM((steps,) + panel.shape, jnp.bfloat16),
-            pltpu.VMEM((3, block, block), jnp.bfloat16),
             pltpu.VMEM((block, block), jnp.bfloat16),
             pltpu.SemaphoreType.DMA((blocks,)),
             pltpu.SemaphoreType.DMA((blocks,)),
@@ -325,9 +359,25 @@
             pltpu.SemaphoreType.DMA((3, PIECES)),
         ],
         compiler_params=pltpu.CompilerParams(
-            collective_id=0, has_side_effects=True, vmem_limit_bytes=56 * 1024 * 1024
+            collective_id=0, has_side_effects=True, vmem_limit_bytes=49 * 1024 * 1024
         ),
     )(panel, rhs, diag_inverse)
+    return pl.pallas_call(
+        writer,
+        out_shape=(
+            jax.ShapeDtypeStruct((steps * block, block), jnp.bfloat16),
+            jax.ShapeDtypeStruct(rhs.shape, jnp.float32),
+        ),
+        in_specs=[pl.BlockSpec(memory_space=pltpu.VMEM)] * 3,
+        out_specs=(pl.BlockSpec(memory_space=pltpu.HBM),) * 2,
+        scratch_shapes=[
+            pltpu.VMEM((2, rhs.shape[0], block // 2), jnp.float32),
+            pltpu.SemaphoreType.DMA((blocks,)),
+            pltpu.SemaphoreType.DMA((2,)),
+            pltpu.SemaphoreType.DMA((2,)),
+        ],
+        compiler_params=pltpu.CompilerParams(vmem_limit_bytes=16 * 1024 * 1024),
+    )(*parts)
 
 
 def solution(mesh):

time: 77.6 us -> 75.7 us (0.976)
  local copies, waits for them, and re-layouts: 3.68 us -> 0 us
  Pallas kernels: 73.1 us -> 74.9 us
    unnamed x2 -> x0, local copies, waits for them, and re-layouts: 3.68 us -> none
    pallas_call x0 -> x1, Pallas kernels: none -> 3.07 us  [shards(): pl.pallas_call(writer, out_shape=(jax.ShapeDtypeStruct((steps * block, bl...]
    pallas_call x1, Pallas kernels: 73.1 us -> 71.8 us  [shards(): pl.pallas_call(functools.partial(kernel, lax.axis_size('col')), out_shape...]
where the time goes in v2:
time: 75.7 us; the launch traced here: 75.5 us
  Pallas kernels  74.9 us (99%)
    pallas_call x1, Pallas kernels, shards(): pl.pallas_call(functools.partial(kernel, lax.axis_size('col')), out_shape...  71.8 us
    pallas_call x1, Pallas kernels, shards(): pl.pallas_call(writer, out_shape=(jax.ShapeDtypeStruct((steps * block, bl...  3.07 us

profile of v2, /device:TPU:12, one launch (start us, length us, event | category | flops | bytes accessed | tf_op | source)
XLA Modules:
  0.0 75.5 jit_solution(9845882908684536776)
XLA Ops:
  0.6 71.8 %shard_map.50 = (f32[512,3072]{1,0:T(8,128)S(1)}, bf16[2,3072,512]{2,1,0:T(8,128)(2,1)S(1)}, bf16[3,512,512]{2,1,0:T(8,128)(2,1)S(1)}) custom-call(bf16[3072,512]{1,0:T(8,128)(2,1)} %panel_hbm.1, f32[512,3072]{1,0:T(8,128)} %rhs_hbm.1, bf16[2,512,512]{2,1,0:T(8,128)(2,1)} %inverse_hbm.1), custom_call_target="tpu_custom_call" | custom-call | tf_op jit(solution)/shard_map/pallas_call | solution.py:342
  72.5 3.1 %shard_map.51 = (bf16[1024,512]{1,0:T(8,128)(2,1)}, f32[512,3072]{1,0:T(8,128)}) custom-call(f32[512,3072]{1,0:T(8,128)S(1)} %get-tuple-element.5.updated_ref, bf16[2,3072,512]{2,1,0:T(8,128)(2,1)S(1)} %get-tuple-element.6.pan, bf16[3,512,512]{2,1,0:T(8,128)(2,1)S(1)} %get-tuple-element.7.quarter), custom_call_target="tpu_custom_call" | custom-call | tf_op jit(solution)/shard_map/pallas_call | solution.py:365

commit v3 on v2

--- a/solution.py
+++ b/solution.py
@@ -14,6 +14,14 @@
 
 def times_transposed(left, right):
     return lax.dot_general(left, right, CONTRACT, preferred_element_type=jnp.float32)
+
+
+def cuts(blocks):
+    return blocks // 2, blocks - 1
+
+
+def only(condition):
+    return (lambda f: f()) if condition is None else pl.when(condition)
 
 
 def solve(residual, inverse):
@@ -31,8 +39,8 @@
     rhs_hbm,
     inverse_hbm,
     updated_ref,
+    quarter,
     pan,
-    quarter,
     inverse_ref,
     load_panel,
     load_rhs,
@@ -44,6 +52,7 @@
 ):
     steps, block = inverse_hbm.shape[0], inverse_hbm.shape[1]
     blocks = panel_hbm.shape[0] // block
+    even_cut, odd_cut = cuts(blocks)
     rows = block // PIECES
     chips = cols // 2
     i = lax.axis_index("row")
@@ -57,6 +66,9 @@
     has_child = chip + 2 < chips
     has_second = root & (chips > 1)
 
+    def mine(j):
+        return None if j < even_cut else core == 1
+
     def dropped(k):
         return (c < steps) & (k >= c)
 
@@ -129,10 +141,12 @@
     def _():
         panel_load(0).start()
 
-    for j in range(1, blocks):
-        panel_load(j).start()
-    for j in range(1, blocks):
-        rhs_load(j).start()
+    for j in range(1, odd_cut):
+
+        @only(mine(j))
+        def _(j=j):
+            panel_load(j).start()
+            rhs_load(j).start()
 
     count = (
         2
@@ -155,9 +169,12 @@
             pan[k, pl.ds(0, block), :] = jnp.zeros((block, block), jnp.bfloat16)
 
     def send_rest():
-        for j in range(1, blocks):
-            panel_load(j).wait()
-            panel_copy(j, i).start()
+        for j in range(1, odd_cut):
+
+            @only(mine(j))
+            def _(j=j):
+                panel_load(j).wait()
+                panel_copy(j, i).start()
 
     pl.when(jnp.logical_not(root))(send_rest)
     inverse_load.wait()
@@ -269,16 +286,18 @@
         update(j)
         return carry
 
-    lax.fori_loop(1, blocks - 1, chunk, 0)
-    rhs_load(blocks - 1).wait()
-    panel_copy(blocks - 1, other).wait_recv()
+    lax.fori_loop(1, jnp.where(core == 1, odd_cut, even_cut), chunk, 0)
 
     @pl.when(jnp.logical_not(dropped(i)))
     def _():
         panel_copy(0, i).wait_send()
 
-    for j in range(1, blocks):
-        panel_copy(j, i).wait_send()
+    for j in range(1, odd_cut):
+
+        @only(mine(j))
+        def _(j=j):
+            panel_copy(j, i).wait_send()
+
     for p in range(PIECES):
 
         @pl.when(is_first)
@@ -299,39 +318,157 @@
                 piece_copy(1, 2, p, 3, (other, 1 - c)).wait_send()
 
 
-def writer(updated_ref, pan, quarter, solved_hbm, updated_hbm, last, done_sem, last_sem, solved_sem):
+def first_writer(blocks, updated_ref, quarter, solved_hbm, updated_hbm, done_sem, solved_sem):
     block = quarter.shape[1]
-    blocks = updated_ref.shape[1] // block
+    even_cut, odd_cut = cuts(blocks)
     i = lax.axis_index("row")
+    core = lax.rem(lax.axis_index("col"), 2)
+
+    def block_put(j):
+        at = pl.ds(j * block, block)
+        return pltpu.make_async_copy(updated_ref.at[:, at], updated_hbm.at[:, at], done_sem.at[j])
+
+    def solved_put(part):
+        slot, half = ((i, i), (2, 1 - i))[part]
+        at = pl.ds(pl.multiple_of(half * block, block), block)
+        return pltpu.make_async_copy(
+            quarter.at[slot], solved_hbm.at[at, :], solved_sem.at[part]
+        )
+
+    for step in ("start", "wait"):
+        for j in range(odd_cut):
+
+            @only(None if j < even_cut else core == 1)
+            def _(j=j, step=step):
+                getattr(block_put(j), step)()
+
+        for part in range(2):
+            getattr(solved_put(part), step)()
+
+
+def second_kernel(
+    panel_hbm,
+    rhs_hbm,
+    quarter,
+    solved_hbm,
+    updated_ref,
+    pan,
+    kept,
+    load_panel,
+    load_rhs,
+    panel_send,
+    panel_recv,
+):
+    block = quarter.shape[1]
+    blocks = panel_hbm.shape[0] // block
+    even_cut, odd_cut = cuts(blocks)
+    i = lax.axis_index("row")
+    c = lax.axis_index("col")
+    other = 1 - i
+    core = lax.rem(c, 2)
+
+    def mine(j):
+        return None if j >= odd_cut else core == 0
+
+    def rhs_load(j):
+        return pltpu.make_async_copy(
+            rhs_hbm.at[:, pl.ds(j * block, block)],
+            updated_ref.at[:, pl.ds((j - even_cut) * block, block)],
+            load_rhs.at[j - even_cut],
+        )
+
+    def panel_load(j):
+        return pltpu.make_async_copy(
+            panel_hbm.at[pl.ds(j * block, block), :],
+            pan.at[i, pl.ds((j - even_cut) * block, block), :],
+            load_panel.at[j - even_cut],
+        )
+
+    def panel_copy(j, which):
+        at = pl.ds((j - even_cut) * block, block)
+        return pltpu.make_async_remote_copy(
+            src_ref=pan.at[which, at, :],
+            dst_ref=pan.at[which, at, :],
+            send_sem=panel_send.at[j - even_cut],
+            recv_sem=panel_recv.at[j - even_cut],
+            device_id=(other, c),
+            device_id_type=MESH,
+        )
+
+    barrier = pltpu.get_barrier_semaphore()
+    pl.semaphore_signal(barrier, inc=1, device_id=(other, c), device_id_type=MESH)
+    for load in (panel_load, rhs_load):
+        for j in range(even_cut, blocks):
+
+            @only(mine(j))
+            def _(j=j, load=load):
+                load(j).start()
+
+    pl.semaphore_wait(barrier, 1)
+    for j in range(even_cut, blocks):
+
+        @only(mine(j))
+        def _(j=j):
+            panel_load(j).wait()
+            panel_copy(j, i).start()
+
+    kept[...] = quarter[pl.ds(0, 2)]
+    for j in range(even_cut, blocks):
+
+        @only(mine(j))
+        def _(j=j):
+            rhs_load(j).wait()
+            panel_copy(j, other).wait_recv()
+            if j < blocks - 1:
+                at = pl.ds((j - even_cut) * block, block)
+                total = times_transposed(quarter[0], pan[0, at, :])
+                total = total + times_transposed(quarter[1], pan[1, at, :])
+                updated_ref[:, at] = updated_ref[:, at] - total
+
+    for j in range(even_cut, blocks):
+
+        @only(mine(j))
+        def _(j=j):
+            panel_copy(j, i).wait_send()
+
+
+def second_writer(blocks, updated_ref, pan, quarter, _, updated_hbm, last, done_sem, last_sem):
+    block = quarter.shape[1]
+    even_cut, odd_cut = cuts(blocks)
+    core = lax.rem(lax.axis_index("col"), 2)
+
+    def block_put(j):
+        return pltpu.make_async_copy(
+            updated_ref.at[:, pl.ds((j - even_cut) * block, block)],
+            updated_hbm.at[:, pl.ds(j * block, block)],
+            done_sem.at[j - even_cut],
+        )
+
+    for j in range(even_cut, odd_cut):
+
+        @pl.when(core == 0)
+        def _(j=j):
+            block_put(j).start()
+
+    width = block // 2
     copies = []
-
-    def put(j):
-        at = pl.ds(j * block, block)
-        copies.append(
-            pltpu.make_async_copy(updated_ref.at[:, at], updated_hbm.at[:, at], done_sem.at[j])
-        )
-        copies[-1].start()
-
-    for j in range(blocks - 1):
-        put(j)
-    for part, slot in enumerate((i, 2)):
-        half = i if part == 0 else 1 - i
-        at = pl.ds(pl.multiple_of(half * block, block), block)
-        copies.append(
-            pltpu.make_async_copy(quarter.at[slot], solved_hbm.at[at, :], solved_sem.at[part])
-        )
-        copies[-1].start()
-    width = block // 2
     for part in range(2):
-        start = (blocks - 1) * block + part * width
+        start = (blocks - 1 - even_cut) * block + part * width
         at = pl.ds(start, width)
         total = times_transposed(quarter[0], pan[0, at, :])
         total = total + times_transposed(quarter[1], pan[1, at, :])
         last[part] = updated_ref[:, at] - total
+        to = pl.ds(start + even_cut * block, width)
         copies.append(
-            pltpu.make_async_copy(last.at[part], updated_hbm.at[:, at], last_sem.at[part])
+            pltpu.make_async_copy(last.at[part], updated_hbm.at[:, to], last_sem.at[part])
         )
         copies[-1].start()
+    for j in range(even_cut, odd_cut):
+
+        @pl.when(core == 0)
+        def _(j=j):
+            block_put(j).wait()
+
     for copy in copies:
         copy.wait()
 
@@ -339,45 +476,73 @@
 def shards(panel, rhs, diag_inverse):
     steps, block = diag_inverse.shape[:2]
     blocks = panel.shape[0] // block
-    parts = pl.pallas_call(
+    even_cut, odd_cut = cuts(blocks)
+    rest = blocks - even_cut
+    hbm = pl.BlockSpec(memory_space=pltpu.HBM)
+    vmem = pl.BlockSpec(memory_space=pltpu.VMEM)
+    dma = pltpu.SemaphoreType.DMA
+    first, quarter = pl.pallas_call(
         functools.partial(kernel, lax.axis_size("col")),
         out_shape=(
-            pltpu.VMEM(rhs.shape, jnp.float32),
-            pltpu.VMEM((steps,) + panel.shape, jnp.bfloat16),
+            pltpu.VMEM((rhs.shape[0], odd_cut * block), jnp.float32),
             pltpu.VMEM((3, block, block), jnp.bfloat16),
         ),
-        in_specs=[pl.BlockSpec(memory_space=pltpu.HBM)] * 3,
-        out_specs=(pl.BlockSpec(memory_space=pltpu.VMEM),) * 3,
+        in_specs=[hbm] * 3,
+        out_specs=(vmem,) * 2,
         scratch_shapes=[
+            pltpu.VMEM((steps, odd_cut * block, block), jnp.bfloat16),
             pltpu.VMEM((block, block), jnp.bfloat16),
-            pltpu.SemaphoreType.DMA((blocks,)),
-            pltpu.SemaphoreType.DMA((blocks,)),
-            pltpu.SemaphoreType.DMA,
-            pltpu.SemaphoreType.DMA((blocks,)),
-            pltpu.SemaphoreType.DMA((blocks,)),
-            pltpu.SemaphoreType.DMA((4, 3, PIECES)),
-            pltpu.SemaphoreType.DMA((3, PIECES)),
+            dma((blocks,)),
+            dma((blocks,)),
+            dma,
+            dma((blocks,)),
+            dma((blocks,)),
+            dma((4, 3, PIECES)),
+            dma((3, PIECES)),
         ],
         compiler_params=pltpu.CompilerParams(
-            collective_id=0, has_side_effects=True, vmem_limit_bytes=49 * 1024 * 1024
+            collective_id=0, has_side_effects=True, vmem_limit_bytes=57 * 1024 * 1024
         ),
     )(panel, rhs, diag_inverse)
-    return pl.pallas_call(
-        writer,
+    solved, updated = pl.pallas_call(
+        functools.partial(first_writer, blocks),
         out_shape=(
             jax.ShapeDtypeStruct((steps * block, block), jnp.bfloat16),
             jax.ShapeDtypeStruct(rhs.shape, jnp.float32),
         ),
-        in_specs=[pl.BlockSpec(memory_space=pltpu.VMEM)] * 3,
-        out_specs=(pl.BlockSpec(memory_space=pltpu.HBM),) * 2,
+        in_specs=[vmem] * 2,
+        out_specs=(hbm,) * 2,
+        scratch_shapes=[dma((blocks,)), dma((2,))],
+        compiler_params=pltpu.CompilerParams(vmem_limit_bytes=16 * 1024 * 1024),
+    )(first, quarter)
+    second, pan, kept = pl.pallas_call(
+        second_kernel,
+        out_shape=(
+            pltpu.VMEM((rhs.shape[0], rest * block), jnp.float32),
+            pltpu.VMEM((steps, rest * block, block), jnp.bfloat16),
+            pltpu.VMEM((2, block, block), jnp.bfloat16),
+        ),
+        in_specs=[hbm, hbm, vmem, hbm],
+        out_specs=(vmem,) * 3,
+        scratch_shapes=[dma((rest,)), dma((rest,)), dma((rest,)), dma((rest,))],
+        compiler_params=pltpu.CompilerParams(
+            collective_id=1, has_side_effects=True, vmem_limit_bytes=54 * 1024 * 1024
+        ),
+    )(panel, rhs, quarter, solved)
+    updated = pl.pallas_call(
+        functools.partial(second_writer, blocks),
+        out_shape=jax.ShapeDtypeStruct(rhs.shape, jnp.float32),
+        in_specs=[vmem] * 3 + [hbm],
+        out_specs=hbm,
         scratch_shapes=[
             pltpu.VMEM((2, rhs.shape[0], block // 2), jnp.float32),
-            pltpu.SemaphoreType.DMA((blocks,)),
-            pltpu.SemaphoreType.DMA((2,)),
-            pltpu.SemaphoreType.DMA((2,)),
+            dma((rest,)),
+            dma((2,)),
         ],
+        input_output_aliases={3: 0},
         compiler_params=pltpu.CompilerParams(vmem_limit_bytes=16 * 1024 * 1024),
-    )(*parts)
+    )(second, pan, kept, updated)
+    return solved, updated
 
 
 def solution(mesh):

time: 75.7 us -> 75.8 us (level)
  the two profiles are of different devices: /device:TPU:12 before, /device:TPU:1 now
where the time goes in v3:
time: 75.8 us; the launch traced here: 75.7 us
  Pallas kernels  74.6 us (98%)
    pallas_call x1, Pallas kernels, shards(): pl.pallas_call(functools.partial(kernel, lax.axis_size('col')), out_shape...  58.1 us
    pallas_call x1, Pallas kernels, shards(): pl.pallas_call(second_kernel, out_shape=(pltpu.VMEM((rhs.shape[0], rest *...  12.1 us
    pallas_call x1, Pallas kernels, shards(): pl.pallas_call(functools.partial(first_writer, blocks), out_shape=(jax.Sh...  2.75 us
    pallas_call x1, Pallas kernels, shards(): pl.pallas_call(functools.partial(second_writer, blocks), out_shape=jax.Sh...  1.76 us

profile of v3, /device:TPU:1, one launch (start us, length us, event | category | flops | bytes accessed | tf_op | source)
XLA Modules:
  0.0 75.7 jit_solution(333862469392794938)
XLA Ops:
  0.6 58.1 %shard_map.50 = (f32[512,2560]{1,0:T(8,128)S(1)}, bf16[3,512,512]{2,1,0:T(8,128)(2,1)S(1)}) custom-call(bf16[3072,512]{1,0:T(8,128)(2,1)} %panel_hbm.3, f32[512,3072]{1,0:T(8,128)} %rhs_hbm.3, bf16[2,512,512]{2,1,0:T(8,128)(2,1)} %inverse_hbm.1), custom_call_target="tpu_custom_call" | custom-call | tf_op jit(solution)/shard_map/pallas_call | solution.py:484
  58.7 0.0 copy-start
  58.7 2.7 %shard_map.51 = (bf16[1024,512]{1,0:T(8,128)(2,1)}, f32[512,3072]{1,0:T(8,128)}) custom-call(f32[512,2560]{1,0:T(8,128)S(1)} %get-tuple-element.9.updated_ref, bf16[3,512,512]{2,1,0:T(8,128)(2,1)S(1)} %get-tuple-element.10.quarter), custom_call_target="tpu_custom_call" | custom-call | tf_op jit(solution)/shard_map/pallas_call | solution.py:507
  61.5 0.4 copy-done
  61.8 12.1 %shard_map.52 = (f32[512,1536]{1,0:T(8,128)S(1)}, bf16[2,1536,512]{2,1,0:T(8,128)(2,1)S(1)}, bf16[2,512,512]{2,1,0:T(8,128)(2,1)S(1)}) custom-call(bf16[3072,512]{1,0:T(8,128)(2,1)} %panel_hbm.3, f32[512,3072]{1,0:T(8,128)} %rhs_hbm.3, bf16[3,512,512]{2,1,0:T(8,128)(2,1)} %copy-done, bf16[1024,512]{1,0:T(8,128)(2,1)} %get-tuple-element.7.solved_hbm), custom_call_target="tpu_custom_call" | custom-call | tf_op jit(solution)/shard_map/pallas_call | solution.py:518
  73.9 1.8 %shard_map.53 = f32[512,3072]{1,0:T(8,128)} custom-call(f32[512,1536]{1,0:T(8,128)S(1)} %get-tuple-element.12.updated_ref, bf16[2,1536,512]{2,1,0:T(8,128)(2,1)S(1)} %get-tuple-element.13.pan, bf16[2,512,512]{2,1,0:T(8,128)(2,1)S(1)} %get-tuple-element.14.quarter, f32[512,3072]{1,0:T(8,128)} %get-tuple-element.15._), custom_call_target="tpu_custom_call", output_to_operand_aliasing={{}: (3, {})} | custom-call | tf_op jit(solution)/shard_map/pallas_call | solution.py:532
Async XLA Ops:
  58.7 3.1 %copy-start = (bf16[3,512,512]{2,1,0:T(8,128)(2,1)}, bf16[3,512,512]{2,1,0:T(8,128)(2,1)S(1)}, u32[]{:S(2)}) copy-start(bf16[3,512,512]{2,1,0:T(8,128)(2,1)S(1)} %get-tuple-element.10.quarter) | copy-start | bytes 4718596
